TPU v7x, 32 devices: a whole 2x2x4 slice. The times are simulated.
32 devices in a mesh: rep: 16 (over z, y, x), shard: 2 (over core).
Axes of the slice: x: 2, y: 2, z: 4, core: 2. Of those that a mesh axis runs over, the one named last changes fastest.
Arguments:
- outer_params: float32 [4, 131072], P('shard'), may hold values from -6 to 6
- replica_delta: float32 [16, 4, 131072], P('rep', 'shard'), may hold values from -20 to 20
- momentum: float32 [4, 131072], P('shard', 'rep'), may hold values from -20 to 20
- tensor_of_block: int32 [4], P('shard'), may hold values from 0 to 1, as said below
Outputs:
- new_params: float32 [4, 131072], P('shard')
- new_momentum: float32 [4, 131072], P('shard', 'rep')
Inputs may be any that keep to these rules, and one draw needn't show every extreme that they name: `tensor_of_block`: every tensor owns exactly 2 blocks.
All inputs are finite; a program needn't handle non-finite values.
Results may differ from a plain program's by a relative error of at most 0.00028.
Values sent between devices are 32-bit elements; how exact they have to be, the bound alone decides.
No kernel may reach another device: no remote copies, remote signals or barrier semaphores. Data moves between devices by JAX's collectives and lax.ppermute only.
A program may use at most 64 MiB of HBM per device.

v0:
```python
import jax
import jax.numpy as jnp
from jax import lax
from jax.sharding import PartitionSpec as P

BLOCK_ROWS = 128
BLOCK_COLS = 1024
NS_STEPS = 8
outer_rate = 0.7
decay_rate = 0.9


def orthogonalize(direction):
    blocks = direction.reshape(direction.shape[0], BLOCK_ROWS, BLOCK_COLS)
    blocks = blocks / jnp.sqrt(jnp.sum(blocks * blocks, axis=(1, 2), keepdims=True) + 1.0)
    for step in range(NS_STEPS):
        square = jnp.einsum("bij,bkj->bik", blocks, blocks, precision=lax.Precision.HIGHEST)
        blocks = 1.5 * blocks - 0.5 * jnp.einsum(
            "bik,bkj->bij", square, blocks, precision=lax.Precision.HIGHEST
        )
    return blocks.reshape(direction.shape[0], BLOCK_ROWS * BLOCK_COLS)


def group_sums(member, param_part, update_part):
    per_block = jnp.stack(
        [jnp.sum(param_part * param_part, axis=1), jnp.sum(update_part * update_part, axis=1)],
        axis=1,
    )
    return jnp.sum(member[:, :, None] * per_block[:, None, :], axis=0)


def block_rates(tensor_sums, member):
    group_rate = outer_rate * jnp.sqrt(
        jnp.maximum(tensor_sums[:, 0], 1.0) / jnp.maximum(tensor_sums[:, 1], 1.0)
    )
    return jnp.sum(member * group_rate[None, :], axis=1)


def shards(outer_params, replica_delta, momentum, tensor_of_block):
    own_delta = replica_delta[0]
    replicas = lax.axis_size("rep")
    all_blocks = tensor_of_block.shape[0] * lax.axis_size("shard")
    tensors = max(all_blocks // 4, 2)
    member = (tensor_of_block[:, None] == jnp.arange(tensors, dtype=jnp.int32)[None, :]).astype(
        jnp.float32
    )
    owned_cols = momentum.shape[1]
    mean_delta = lax.psum(own_delta, "rep") / replicas
    whole_moment = lax.all_gather(momentum, "rep", axis=1, tiled=True)
    new_whole = decay_rate * whole_moment + mean_delta
    direction = mean_delta + decay_rate * new_whole
    update = orthogonalize(direction)
    tensor_sums = lax.psum(group_sums(member, outer_params, update), "shard")
    new_momentum = lax.dynamic_slice_in_dim(
        new_whole, lax.axis_index("rep") * owned_cols, owned_cols, 1
    )
    block_rate = block_rates(tensor_sums, member)
    new_params = outer_params - block_rate[:, None] * update
    return (new_params, new_momentum)


def solution(mesh):
    return jax.shard_map(
        shards,
        mesh=mesh,
        in_specs=(P("shard", None), P("rep", "shard", None), P("shard", "rep"), P("shard")),
        out_specs=(P("shard", None), P("shard", "rep")),
        check_vma=False,
    )
```

profile of v0, /device:TPU:0, one launch (start us, length us, event | category | flops | bytes accessed | tf_op | source)
XLA Modules:
  0.0 222.0 jit_solution(5751966539528408247)
XLA Ops:
  7.2 0.7 all-reduce.2.cloned.1.call-update
  7.9 0.0 all-gather.2.cloned.1.call-start
  8.0 0.7 all-gather.2.cloned.1.call-update
  8.7 1.2 multiply_reduce_fusion.2
  9.9 0.1 fusion.9
  9.9 118.5 %all-reduce.2.cloned.1.call-done = f32[2,131072]{1,0:T(2,128)} async-done(((f32[2,131072]{1,0:T(2,128)}), f32[2,131072]{1,0:T(2,128)}) %all-reduce.2.cloned.1.call-update) | async-done | bytes 1048592 | tf_op jit(solution)/shard_map/psum | solution.py:48
  128.5 57.0 %all-gather.2.cloned.1.call-done = f32[2,131072]{1,0:T(2,128)} async-done(((f32[2,8192]{1,0:T(2,128)}), f32[2,131072]{1,0:T(2,128)}) %all-gather.2.cloned.1.call-update) | async-done | bytes 1048592 | tf_op jit(solution)/shard_map/all_gather | solution.py:49
  185.4 3.9 %multiply_reduce_fusion.1 = (f32[2]{0:T(128)S(1)}, f32[2,131072]{1,0:T(2,128)S(1)}, f32[2,131072]{1,0:T(2,128)}) fusion(f32[2,131072]{1,0:T(2,128)} %all-gather.2.cloned.1.call-done, f32[2,131072]{1,0:T(2,128)} %all-reduce.2.cloned.1.call-done), kind=kLoop, calls=%fused_computation.19 | loop fusion | flops 1835006 | bytes 4194312 | tf_op jit(solution)/shard_map/reduce_sum | solution.py:15
  189.3 1.7 fusion.8
  191.1 1.6 fusion.7
  192.7 1.1 fusion.10
  193.8 1.1 fusion.6
  194.8 1.1 fusion.11
  195.9 1.1 fusion.5
  197.0 1.1 fusion.12
  198.1 1.1 fusion.4
  199.2 1.3 fusion.13
  200.5 1.1 fusion.3
  201.5 1.1 fusion.14
  202.6 1.1 fusion.2
  203.7 1.1 fusion.15
  204.8 1.1 fusion.1
  205.8 1.1 fusion.16
  206.9 1.2 multiply_reduce_fusion
  208.2 0.1 copy.8
  208.3 0.1 multiply_reduce_fusion.3
  208.4 0.8 copy.10
  209.2 2.5 %psum.15 = f32[2,2]{1,0:T(2,128)S(1)} all-reduce(f32[2,2]{1,0:T(2,128)S(1)} %multiply_reduce_fusion.3), channel_id=1, replica_groups=mesh['rep'=16,'shard'=2] {'shard'}, use_global_device_ids=true, to_apply=%region_5.0 | all-reduce | flops 4 | bytes 32 | tf_op jit(solution)/shard_map/psum | solution.py:53
  211.7 0.2 multiply_reduce_fusion.4
  211.9 0.2 select_reduce_fusion
  212.1 1.6 multiply_subtract_fusion
  213.6 1.5 constant_dynamic-slice_fusion
  (7 shorter events, 0.1 us)
Async XLA Ops:
  7.2 1.5 copy-start
  7.2 121.3 %all-reduce.2.cloned.1.call-start = ((), (), s32[]{:S(2)}) async-start(), calls=%async_computation | async-start | bytes 2097152 | tf_op jit(solution)/shard_map/psum | solution.py:48
  7.9 177.5 %all-gather.2.cloned.1.call-start = ((), (), s32[]{:S(2)}) async-start(), calls=%async_computation.1 | async-start | bytes 1114112 | tf_op jit(solution)/shard_map/all_gather | solution.py:49
  8.7 1.2 copy-start.1
Sparse Core Ops, SparseCore 0:
  13.3 115.1 all-reduce.1
  131.2 54.1 all-gather.1
where the time goes:
time: 222 us
  waiting for transfers between devices  177 us (80%)
  matrix products  18.7 us (8%)
  between operations  14.2 us (6%)
  other arithmetic  7.22 us (3%)
  blocking collectives  2.47 us (1%)
  local copies, waits for them, and re-layouts  2.39 us (1%)
    psum x1, waiting for transfers between devices, shards(): mean_delta = lax.psum(own_delta, 'rep') / replicas  119 us
    all_gather x1, waiting for transfers between devices, shards(): whole_moment = lax.all_gather(momentum, 'rep', axis=1, tiled=True)  57 us
    dot_general x8, matrix products, orthogonalize(): jnp.einsum('bij,bkj->bik', blocks, blocks, precision=lax.Precision.HIGHEST)  9.57 us
    dot_general x8, matrix products, orthogonalize(): jnp.einsum('bik,bkj->bij', square, blocks, precision=lax.Precision.HIGHEST)  9.17 us
  transfers between devices with their start and end apart: 2, of which 2 were waited for; matrix products, arithmetic and copies ran while one was open for 1% of the time, Pallas kernels for 0%

commit v1 on v0

--- a/solution.py
+++ b/solution.py
@@ -45,7 +45,7 @@
         jnp.float32
     )
     owned_cols = momentum.shape[1]
-    mean_delta = lax.psum(own_delta, "rep") / replicas
+    mean_delta = jnp.sum(lax.all_gather(own_delta, "rep"), axis=0) / replicas
     whole_moment = lax.all_gather(momentum, "rep", axis=1, tiled=True)
     new_whole = decay_rate * whole_moment + mean_delta
     direction = mean_delta + decay_rate * new_whole

time: 222 us -> 297 us (1.34)
  waiting for transfers between devices: 177 us -> 243 us
  other arithmetic: 7.22 us -> 15.9 us
    all_gather x0 -> x1, waiting for transfers between devices: none -> 193 us  [shards(): mean_delta = jnp.sum(lax.all_gather(own_delta, 'rep'), axis=0) / replicas]
    psum x1 -> x0, waiting for transfers between devices: 119 us -> none  [shards(): mean_delta = lax.psum(own_delta, 'rep') / replicas]
    all_gather x1, waiting for transfers between devices: 57 us -> 48.9 us  [shards(): whole_moment = lax.all_gather(momentum, 'rep', axis=1, tiled=True)]
    reduce_sum x0 -> x1, other arithmetic: none -> 7.12 us  [shards(): mean_delta = jnp.sum(lax.all_gather(own_delta, 'rep'), axis=0) / replicas]
  transfers between devices with their start and end apart: 2 -> 2, of which waited for: 2 -> 2; matrix products, arithmetic and copies ran while one was open for 1% -> 3% of each run, Pallas kernels for 0% -> 0%
where the time goes in v1:
time: 297 us
  waiting for transfers between devices  243 us (82%)
  matrix products  18.7 us (6%)
  other arithmetic  15.9 us (5%)
  between operations  14.2 us (5%)
    all_gather x1, waiting for transfers between devices, shards(): mean_delta = jnp.sum(lax.all_gather(own_delta, 'rep'), axis=0) / replicas  193 us
    all_gather x1, waiting for transfers between devices, shards(): whole_moment = lax.all_gather(momentum, 'rep', axis=1, tiled=True)  48.9 us
    dot_general x8, matrix products, orthogonalize(): jnp.einsum('bij,bkj->bik', blocks, blocks, precision=lax.Precision.HIGHEST)  9.54 us
    dot_general x8, matrix products, orthogonalize(): jnp.einsum('bik,bkj->bij', square, blocks, precision=lax.Precision.HIGHEST)  9.17 us
    reduce_sum x1, other arithmetic, shards(): mean_delta = jnp.sum(lax.all_gather(own_delta, 'rep'), axis=0) / replicas  7.12 us
  transfers between devices with their start and end apart: 2, of which 2 were waited for; matrix products, arithmetic and copies ran while one was open for 3% of the time, Pallas kernels for 0%

profile of v1, /device:TPU:0, one launch (start us, length us, event | category | flops | bytes accessed | tf_op | source)
XLA Modules:
  0.0 296.8 jit_solution(15904611502925311571)
XLA Ops:
  7.2 0.7 all-gather.3.cloned.1.call-update
  7.9 0.7 all-gather.5.cloned.1.call-update
  8.7 2.4 multiply_reduce_fusion.2
  11.1 0.7 fusion.9
  11.8 192.7 %all-gather.3.cloned.1.call-done = f32[16,2,131072]{2,1,0:T(2,128)} async-done(((f32[1,2,131072]{2,1,0:T(2,128)}), f32[16,2,131072]{2,1,0:T(2,128)}) %all-gather.3.cloned.1.call-update) | async-done | bytes 16777232 | tf_op jit(solution)/shard_map/all_gather | solution.py:48
  204.5 7.1 %reduce_sum.55 = f32[2,131072]{1,0:T(2,128)S(1)} reduce(f32[16,2,131072]{2,1,0:T(2,128)} %all-gather.3.cloned.1.call-done, f32[]{:T(128)} %constant.12.clone.1), dimensions={0}, to_apply=%region_1.0 | reduce | flops 3932160 | bytes 17825796 | tf_op jit(solution)/shard_map/reduce_sum | solution.py:48
  211.6 48.9 %all-gather.5.cloned.1.call-done = f32[2,131072]{1,0:T(2,128)} async-done(((f32[2,8192]{1,0:T(2,128)}), f32[2,131072]{1,0:T(2,128)}) %all-gather.5.cloned.1.call-update) | async-done | bytes 1048592 | tf_op jit(solution)/shard_map/all_gather | solution.py:49
  260.6 3.6 %multiply_reduce_fusion.1 = (f32[2]{0:T(128)S(1)}, f32[2,131072]{1,0:T(2,128)S(1)}, f32[2,131072]{1,0:T(2,128)}) fusion(f32[2,131072]{1,0:T(2,128)} %all-gather.5.cloned.1.call-done, f32[2,131072]{1,0:T(2,128)S(1)} %reduce_sum.55), kind=kLoop, calls=%fused_computation.19 | loop fusion | flops 1835006 | bytes 4194312 | tf_op jit(solution)/shard_map/reduce_sum | solution.py:15
  264.1 1.7 fusion.8
  265.9 1.6 fusion.7
  267.5 1.1 fusion.10
  268.6 1.1 fusion.6
  269.7 1.1 fusion.11
  270.8 1.1 fusion.5
  271.8 1.1 fusion.12
  272.9 1.1 fusion.4
  274.0 1.3 fusion.13
  275.3 1.1 fusion.3
  276.3 1.1 fusion.14
  277.4 1.1 fusion.2
  278.5 1.1 fusion.15
  279.6 1.1 fusion.1
  280.6 1.1 fusion.16
  281.7 1.2 multiply_reduce_fusion
  283.0 0.1 copy.9
  283.1 0.1 multiply_reduce_fusion.3
  283.2 0.8 copy.11
  284.0 2.5 psum.7
  286.5 0.2 multiply_reduce_fusion.4
  286.7 0.2 select_reduce_fusion
  286.9 1.6 multiply_subtract_fusion
  288.4 1.5 constant_dynamic-slice_fusion
  (8 shorter events, 0.1 us)
Async XLA Ops:
  7.2 197.3 %all-gather.3.cloned.1.call-start = ((), (), s32[]{:S(2)}) async-start(), calls=%async_computation | async-start | bytes 17825792 | tf_op jit(solution)/shard_map/all_gather | solution.py:48
  7.9 252.7 %all-gather.5.cloned.1.call-start = ((), (), s32[]{:S(2)}) async-start(), calls=%async_computation.1 | async-start | bytes 1114112 | tf_op jit(solution)/shard_map/all_gather | solution.py:49
  267.5 19.2 %copy-start.1 = (s32[2]{0:T(128)S(1)}, s32[2]{0:T(128)}, u32[]{:S(2)}) copy-start(s32[2]{0:T(128)} %param.7) | copy-start | bytes 28
  267.5 19.4 %copy-start = (f32[2,131072]{1,0:T(2,128)S(1)}, f32[2,131072]{1,0:T(2,128)}, u32[]{:S(2)}) copy-start(f32[2,131072]{1,0:T(2,128)} %param.4) | copy-start | bytes 3145732
Sparse Core Ops, SparseCore 0:
  10.7 193.7 all-gather.2
  207.2 53.2 all-gather.4
